TPU v7x, 32 devices: a whole 2x2x4 slice. The times are simulated.
32 devices in a mesh: dp: 8 (over y, x, core), mp: 4 (over z).
Axes of the slice: x: 2, y: 2, z: 4, core: 2. Of those that a mesh axis runs over, the one named last changes fastest.
Arguments:
- tokens: bfloat16 [8192, 2048], P('dp'), may hold values from -6 to 6
- cotangent: bfloat16 [8192, 2048], P('dp'), may hold values from -6 to 6
- counts: int32 [8], replicated, may hold values from 1 to 1024, 5120 in all
- w_qkv: bfloat16 [2048, 3, 2048], P('dp', None, 'mp'), may hold values from -0.125 to 0.125
- w_out: bfloat16 [2048, 2048], P('mp', 'dp'), may hold values from -1 to 1
- w_fc1: bfloat16 [2048, 8192], P('dp', 'mp'), may hold values from -0.125 to 0.125
- w_fc2: bfloat16 [8192, 2048], P('mp', 'dp'), may hold values from -0.0625 to 0.0625
- ln1_gain: bfloat16 [2048], P('dp'), may hold values from 0.5 to 1.5
- ln1_bias: bfloat16 [2048], P('dp'), may hold values from -1.796875 to 1.796875
- ln2_gain: bfloat16 [2048], P('dp'), may hold values from 0.5 to 1.5
- ln2_bias: bfloat16 [2048], P('dp'), may hold values from -1.796875 to 1.796875
- qv_bias: bfloat16 [2, 2048], P(None, ('mp', 'dp')), may hold values from -1.796875 to 1.796875
- out_bias: bfloat16 [2048], P('dp'), may hold values from -1.796875 to 1.796875
- fc1_bias: bfloat16 [8192], P(('mp', 'dp')), may hold values from -1.796875 to 1.796875
- fc2_bias: bfloat16 [2048], P('dp'), may hold values from -1.796875 to 1.796875
Outputs:
- out_tokens: bfloat16 [8192, 2048], P('dp')
- grad_tokens: float32 [8192, 2048], P('dp')
- grad_w_qkv: float32 [2048, 3, 2048], P('dp', None, 'mp')
- grad_w_out: float32 [2048, 2048], P('mp', 'dp')
- grad_w_fc1: float32 [2048, 8192], P('dp', 'mp')
- grad_w_fc2: float32 [8192, 2048], P('mp', 'dp')
- grad_ln1_gain: float32 [2048], P('dp')
- grad_ln1_bias: float32 [2048], P('dp')
- grad_ln2_gain: float32 [2048], P('dp')
- grad_ln2_bias: float32 [2048], P('dp')
- grad_qv_bias: float32 [2, 2048], P(None, ('mp', 'dp'))
- grad_out_bias: float32 [2048], P('dp')
- grad_fc1_bias: float32 [8192], P(('mp', 'dp'))
- grad_fc2_bias: float32 [2048], P('dp')
Inputs may be any that keep to these rules, and one draw needn't show every extreme that they name: counts[g] is the number of live tokens of group g's sequence, at the start of its 1024 slots; the largest count equals 1024.
All inputs are finite; a program needn't handle non-finite values.
Results may differ from a plain program's by a relative error of at most 0.014.
Values may be sent and summed in bfloat16 or wider, within the bound.
A program may use at most 192 MiB of HBM per device.

v0:
```python
import math
import jax
import jax.numpy as jnp
from jax import lax
from jax.sharding import PartitionSpec as P

HEAD = 128
EPS = 1e-05
NEG = -1e30


def layer_norm(values, gain_vec, shift_vec):
    center = values - jnp.mean(values, axis=-1, keepdims=True)
    spread = jnp.mean(center * center, axis=-1, keepdims=True)
    return center * lax.rsqrt(spread + EPS) * gain_vec + shift_vec


def smooth_gate(values):
    return jax.nn.gelu(values, approximate=True)


def causal_scores(queries, key_heads, inv_root):
    row_count = queries.shape[0]
    raw_scores = (
        jnp.einsum("qhd,khd->hqk", queries, key_heads, preferred_element_type=jnp.float32)
        * inv_root
    )
    future = lax.broadcasted_iota(jnp.int32, (row_count, row_count), 1) > lax.broadcasted_iota(
        jnp.int32, (row_count, row_count), 0
    )
    return jnp.where(future[None], NEG, raw_scores)


def shards(
    tokens,
    cotangent,
    counts,
    w_qkv,
    w_out,
    w_fc1,
    w_fc2,
    ln1_gain,
    ln1_bias,
    ln2_gain,
    ln2_bias,
    qv_bias,
    out_bias,
    fc1_bias,
    fc2_bias,
):
    whole_qkv = lax.all_gather(w_qkv, "dp", axis=0, tiled=True)
    whole_out = lax.all_gather(w_out, "dp", axis=1, tiled=True)
    whole_fc1 = lax.all_gather(w_fc1, "dp", axis=0, tiled=True)
    whole_fc2 = lax.all_gather(w_fc2, "dp", axis=1, tiled=True)
    vectors = (
        ln1_gain,
        ln1_bias,
        ln2_gain,
        ln2_bias,
        out_bias,
        fc2_bias,
        fc1_bias,
        qv_bias.reshape(-1),
    )
    packed = lax.all_gather(jnp.concatenate(vectors), "dp", axis=0).astype(jnp.float32)
    wide = []
    at = 0
    for vector in vectors:
        wide.append(packed[:, at : at + vector.shape[0]])
        at += vector.shape[0]
    gain_one, shift_one, gain_two, shift_two, bias_out, bias_fc2, bias_fc1 = (
        part.reshape(-1) for part in wide[:7]
    )
    n_dp = packed.shape[0]
    bias_qv = wide[7].reshape(n_dp, 2, -1).transpose(1, 0, 2).reshape(2, -1)
    seq_rows = tokens.shape[0]
    local_width = whole_qkv.shape[2]
    heads_here = local_width // HEAD
    inv_root = 1.0 / math.sqrt(HEAD)
    inputs = tokens.astype(jnp.float32)
    normed_one = layer_norm(inputs, gain_one, shift_one).astype(jnp.bfloat16)
    projected = jnp.einsum("sd,dce->sce", normed_one, whole_qkv, preferred_element_type=jnp.float32)
    queries = (
        (projected[:, 0] + bias_qv[0]).astype(jnp.bfloat16).reshape(seq_rows, heads_here, HEAD)
    )
    key_heads = projected[:, 1].astype(jnp.bfloat16).reshape(seq_rows, heads_here, HEAD)
    values = (projected[:, 2] + bias_qv[1]).astype(jnp.bfloat16).reshape(seq_rows, heads_here, HEAD)
    scores = causal_scores(queries, key_heads, inv_root)
    row_peak = jnp.max(scores, axis=-1, keepdims=True)
    exp_terms = jnp.exp(scores - row_peak)
    exp_total = jnp.sum(exp_terms, axis=-1, keepdims=True)
    log_total = row_peak + jnp.log(exp_total)
    prob_low = (exp_terms / exp_total).astype(jnp.bfloat16)
    mixed_heads = (
        jnp.einsum("hqk,khd->qhd", prob_low, values, preferred_element_type=jnp.float32)
        .astype(jnp.bfloat16)
        .reshape(seq_rows, local_width)
    )
    attn_part = jnp.dot(mixed_heads, whole_out, preferred_element_type=jnp.float32)
    residual = (
        inputs + lax.psum(attn_part.astype(jnp.bfloat16), "mp").astype(jnp.float32) + bias_out
    )
    normed_two = layer_norm(residual, gain_two, shift_two).astype(jnp.bfloat16)
    preact = jnp.dot(normed_two, whole_fc1, preferred_element_type=jnp.float32) + bias_fc1
    activated = smooth_gate(preact).astype(jnp.bfloat16)
    ffn_part = jnp.dot(activated, whole_fc2, preferred_element_type=jnp.float32)
    out_tokens = (
        residual + lax.psum(ffn_part.astype(jnp.bfloat16), "mp").astype(jnp.float32) + bias_fc2
    ).astype(jnp.bfloat16)
    dp_index = lax.axis_index("dp")
    slot_ids = lax.iota(jnp.int32, counts.shape[0])
    own_count = jnp.sum(jnp.where(slot_ids == dp_index, counts, 0))
    weight_share = own_count.astype(jnp.float32) / jnp.sum(counts).astype(jnp.float32)
    live_rows = lax.iota(jnp.int32, seq_rows) < own_count
    grad_out = jnp.where(live_rows[:, None], cotangent.astype(jnp.float32), 0.0)
    grad_out_low = grad_out.astype(jnp.bfloat16)
    grad_fc2 = (
        jnp.einsum("sf,sd->fd", activated, grad_out_low, preferred_element_type=jnp.float32)
        * weight_share
    )
    grad_fc2_bias = jnp.sum(grad_out, axis=0) * weight_share
    delta_act = jnp.einsum("sd,fd->sf", grad_out_low, whole_fc2, preferred_element_type=jnp.float32)
    unused_gate, gate_back = jax.vjp(smooth_gate, preact)
    delta_pre = gate_back(delta_act)[0]
    grad_fc1_bias = jnp.sum(delta_pre, axis=0) * weight_share
    delta_pre_low = delta_pre.astype(jnp.bfloat16)
    grad_fc1 = (
        jnp.einsum("sd,sf->df", normed_two, delta_pre_low, preferred_element_type=jnp.float32)
        * weight_share
    )
    two_part = jnp.einsum("sf,df->sd", delta_pre_low, whole_fc1, preferred_element_type=jnp.float32)
    delta_two = lax.psum(two_part.astype(jnp.bfloat16), "mp").astype(jnp.float32)
    unused_two, second_back = jax.vjp(layer_norm, residual, gain_two, shift_two)
    resid_part, gain_two_part, shift_two_part = second_back(delta_two)
    delta_resid = resid_part + grad_out
    delta_resid_low = delta_resid.astype(jnp.bfloat16)
    out_bias_part = jnp.sum(delta_resid, axis=0)
    grad_out_proj = (
        jnp.einsum("sc,sd->cd", mixed_heads, delta_resid_low, preferred_element_type=jnp.float32)
        * weight_share
    )
    delta_mixed = jnp.einsum(
        "sd,cd->sc", delta_resid_low, whole_out, preferred_element_type=jnp.float32
    )
    delta_mixed_low = delta_mixed.astype(jnp.bfloat16).reshape(seq_rows, heads_here, HEAD)
    scores_again = causal_scores(queries, key_heads, inv_root)
    prob_full = jnp.exp(scores_again - log_total)
    delta_prob = jnp.einsum(
        "qhd,khd->hqk", delta_mixed_low, values, preferred_element_type=jnp.float32
    )
    delta_scores = prob_full * (
        delta_prob - jnp.sum(prob_full * delta_prob, axis=-1, keepdims=True)
    )
    delta_scores_low = delta_scores.astype(jnp.bfloat16)
    delta_q = (
        jnp.einsum("hqk,khd->qhd", delta_scores_low, key_heads, preferred_element_type=jnp.float32)
        * inv_root
    ).reshape(seq_rows, local_width)
    delta_k = (
        jnp.einsum("hqk,qhd->khd", delta_scores_low, queries, preferred_element_type=jnp.float32)
        * inv_root
    ).reshape(seq_rows, local_width)
    delta_v = jnp.einsum(
        "hqk,qhd->khd", prob_low, delta_mixed_low, preferred_element_type=jnp.float32
    ).reshape(seq_rows, local_width)
    grad_qv = jnp.stack([jnp.sum(delta_q, axis=0), jnp.sum(delta_v, axis=0)]) * weight_share
    delta_proj = jnp.stack([delta_q, delta_k, delta_v], axis=1).astype(jnp.bfloat16)
    grad_qkv = (
        jnp.einsum("sd,sce->dce", normed_one, delta_proj, preferred_element_type=jnp.float32)
        * weight_share
    )
    one_part = jnp.einsum("sce,dce->sd", delta_proj, whole_qkv, preferred_element_type=jnp.float32)
    delta_one = lax.psum(one_part.astype(jnp.bfloat16), "mp").astype(jnp.float32)
    unused_one, first_back = jax.vjp(layer_norm, inputs, gain_one, shift_one)
    input_part, gain_one_part, shift_one_part = first_back(delta_one)
    grad_tokens = input_part + delta_resid
    grad_vectors = (
        gain_one_part * weight_share,
        shift_one_part * weight_share,
        gain_two_part * weight_share,
        shift_two_part * weight_share,
        out_bias_part * weight_share,
        grad_fc2_bias,
        grad_fc1_bias,
    )
    stacked = jnp.concatenate(
        [vector.reshape(n_dp, -1) for vector in grad_vectors]
        + [grad_qv.reshape(2, n_dp, -1).transpose(1, 0, 2).reshape(n_dp, -1)],
        axis=1,
    )
    own = lax.psum_scatter(stacked, "dp", scatter_dimension=0, tiled=True)[0]
    pieces = []
    at = 0
    for vector in vectors:
        pieces.append(own[at : at + vector.shape[0]])
        at += vector.shape[0]

    def scatter(grad, axis):
        low = grad.astype(jnp.bfloat16)
        return lax.psum_scatter(low, "dp", scatter_dimension=axis, tiled=True).astype(jnp.float32)

    return (
        out_tokens,
        grad_tokens,
        scatter(grad_qkv, 0),
        scatter(grad_out_proj, 1),
        scatter(grad_fc1, 0),
        scatter(grad_fc2, 1),
        pieces[0],
        pieces[1],
        pieces[2],
        pieces[3],
        pieces[7].reshape(2, -1),
        pieces[4],
        pieces[6],
        pieces[5],
    )


def solution(mesh):
    placed = (
        P("dp", None),
        P("dp", None),
        P(),
        P("dp", None, "mp"),
        P("mp", "dp"),
        P("dp", "mp"),
        P("mp", "dp"),
        P("dp"),
        P("dp"),
        P("dp"),
        P("dp"),
        P(None, ("mp", "dp")),
        P("dp"),
        P(("mp", "dp")),
        P("dp"),
    )
    return jax.shard_map(
        shards,
        mesh=mesh,
        in_specs=placed,
        out_specs=(
            P("dp", None),
            P("dp", None),
            P("dp", None, "mp"),
            P("mp", "dp"),
            P("dp", "mp"),
            P("mp", "dp"),
            P("dp"),
            P("dp"),
            P("dp"),
            P("dp"),
            P(None, ("mp", "dp")),
            P("dp"),
            P(("mp", "dp")),
            P("dp"),
        ),
        check_vma=False,
    )
```

profile of v0, /device:TPU:0, one launch (start us, length us, event | category | flops | bytes accessed | tf_op | source)
XLA Modules:
  0.0 1186.2 jit_solution(16017044724826769908)
XLA Ops:
  7.2 2.3 copy.59
  17.1 11.2 all-gather.1
  29.2 2.8 convert_reduce_fusion.2
  33.9 26.1 %all-gather.7.cloned.1.call-done = bf16[2048,3,512]{0,2,1:T(8,128)(2,1)} async-done(((bf16[256,3,512]{0,2,1:T(8,128)(2,1)}), bf16[2048,3,512]{0,2,1:T(8,128)(2,1)}) %all-gather.7.cloned.1.call-update) | async-done | bytes 6291472 | tf_op jit(solution)/shard_map/all_gather | solution.py:51
  60.0 10.4 fusion.43
  72.3 7.7 fusion.62
  80.0 8.1 fusion
  90.1 7.4 divide_convert_fusion
  97.6 3.2 copy-done.6
  102.3 6.0 convolution_convert_fusion.2
  110.9 152.8 %all-reduce.6.cloned.1.call-done = bf16[1024,2048]{1,0:T(8,128)(2,1)} async-done(((bf16[1024,2048]{1,0:T(8,128)(2,1)}), bf16[1024,2048]{1,0:T(8,128)(2,1)}) %all-reduce.6.cloned.1.call-update) | async-done | bytes 4194320 | tf_op jit(solution)/shard_map/psum | solution.py:101
  263.7 5.0 fusion.26
  269.6 2.4 multiply_reduce_fusion.1
  272.0 46.6 %all-gather.11.cloned.1.call-done = bf16[2048,2048]{1,0:T(8,128)(2,1)} async-done(((bf16[256,2048]{1,0:T(8,128)(2,1)}), bf16[2048,2048]{1,0:T(8,128)(2,1)}) %all-gather.11.cloned.1.call-update) | async-done | bytes 8388624 | tf_op jit(solution)/shard_map/all_gather | solution.py:53
  318.7 16.2 %fusion.55 = f32[1024,2048]{1,0:T(8,128)} fusion(bf16[2048,2048]{1,0:T(8,128)(2,1)} %all-gather.11.cloned.1.call-done, f32[2048]{0:T(1024)S(1)} %bitcast.118, f32[2048]{0:T(1024)S(1)} %bitcast.109, f32[1024]{0:T(1024)S(1)} %fusion.48, bf16[1024,2048]{1,0:T(8,128)(2,1)} %all-reduce.6.cloned.1.call-done, bf16[1024,2048]{1,0:T(8,128)(2,1)} %param.15, ...), kind=kOutput, calls=%fused_computation.131 | convolution fusion | flops 8608808960 | bytes 25198592 | tf_op jit(solution)/shard_map/dot_general | solution.py:104
  334.8 41.4 %all-gather.13.cloned.1.call-done = bf16[2048,2048]{1,0:T(8,128)(2,1)} async-done(((bf16[2048,256]{1,0:T(8,128)(2,1)}), bf16[2048,2048]{1,0:T(8,128)(2,1)}) %all-gather.13.cloned.1.call-update) | async-done | bytes 8388624 | tf_op jit(solution)/shard_map/all_gather | solution.py:54
  376.3 20.5 %fusion.63 = (f32[2048]{0:T(1024)}, bf16[1024,2048]{1,0:T(8,128)(2,1)S(1)}) fusion(f32[1024,2048]{1,0:T(8,128)} %fusion.55, f32[2048]{0:T(1024)S(1)} %bitcast.120, bf16[2048,2048]{1,0:T(8,128)(2,1)} %all-gather.13.cloned.1.call-done, bf16[1024,2048]{1,0:T(8,128)(2,1)} %param.16, pred[1024]{0:T(1024)(128)(4,1)S(1)} %iota_compare_fusion.1), kind=kOutput, calls=%fused_computation.137 | convolution fusion | flops 8642361344 | bytes 25183232 | tf_op jit(solution)/shard_map/sd,fd->sf/dot_general | solution.py:122
  398.8 23.0 %convolution_convert_fusion = bf16[1024,2048]{1,0:T(8,128)(2,1)} fusion(bf16[2048,2048]{1,0:T(8,128)(2,1)} %all-gather.11.cloned.1.call-done, bf16[1024,2048]{1,0:T(8,128)(2,1)S(1)} %get-tuple-element.58), kind=kOutput, calls=%fused_computation.61 | convolution fusion | flops 8592031744 | bytes 16777216 | tf_op jit(solution)/shard_map/sf,df->sd/dot_general | solution.py:131
  423.2 16.6 %convolution_convert_fusion.1 = bf16[1024,2048]{1,0:T(8,128)(2,1)} fusion(bf16[2048,2048]{1,0:T(8,128)(2,1)} %all-gather.13.cloned.1.call-done, f32[1024,2048]{1,0:T(8,128)} %fusion.55, f32[2048]{0:T(1024)S(1)} %bitcast.121), kind=kOutput, calls=%fused_computation.62 | convolution fusion | flops 8613003264 | bytes 20979712 | tf_op jit(solution)/shard_map/dot_general | solution.py:106
  439.8 137.2 %all-reduce.8.cloned.1.call-done = bf16[1024,2048]{1,0:T(8,128)(2,1)} async-done(((bf16[1024,2048]{1,0:T(8,128)(2,1)}), bf16[1024,2048]{1,0:T(8,128)(2,1)}) %all-reduce.8.cloned.1.call-update) | async-done | bytes 4194320 | tf_op jit(solution)/shard_map/psum | solution.py:132
  577.0 7.6 convert_reduce_fusion.1
  585.3 5.5 fusion.21
  590.8 5.7 fusion.59
  596.5 3.2 copy-done.9
  599.7 3.7 multiply_convert_fusion.5
  603.8 6.3 fusion.39
  610.2 12.3 %multiply_reduce_fusion = (f32[4,1024]{1,0:T(4,128)S(1)}, f32[4,1024,1024]{1,2,0:T(8,128)}) fusion(f32[4,1024,1024]{1,2,0:T(8,128)} %get-tuple-element.50, f32[4,1024]{1,0:T(4,128)S(1)} %log_add_fusion, bf16[1024,4,128]{0,2,1:T(8,128)(2,1)S(1)} %bitcast.87, f32[1024,4,128]{2,0,1:T(8,128)S(1)} %copy.60, f32[4,128]{1,0:T(4,128)S(1)} %add.145), kind=kOutput, calls=%fused_computation.3 | convolution fusion | flops 1087369216 | bytes 36734976 | tf_op jit(solution)/shard_map/qhd,khd->hqk/dot_general | solution.py:148
  622.4 15.9 %multiply_convert_fusion.2 = bf16[4,1024,1024]{1,2,0:T(8,128)(2,1)} fusion(f32[4,1024,1024]{1,2,0:T(8,128)} %get-tuple-element.54, f32[4,1024,1024]{1,2,0:T(8,128)} %get-tuple-element.50, f32[4,1024]{1,0:T(4,128)S(1)} %get-tuple-element.53, f32[4,1024]{1,0:T(4,128)S(1)} %log_add_fusion), kind=kLoop, calls=%fused_computation.2 | loop fusion | flops 16777216 | bytes 41975808 | tf_op jit(solution)/shard_map/convert_element_type | solution.py:154
  638.4 4.6 bitcast_convert_fusion.1
  642.9 2.5 copy.71
  645.5 6.4 bitcast_convert_fusion.2
  651.8 2.3 copy.69
  654.1 6.3 multiply_convert_fusion.6
  660.9 11.0 bitcast_convert_fusion
  672.0 16.4 %multiply_convert_fusion = bf16[2048,2048]{1,0:T(8,128)(2,1)} fusion(f32[]{:T(128)S(6)} %div.63, bf16[1024,2048]{1,0:T(8,128)(2,1)} %param.16, pred[1024]{0:T(1024)(128)(4,1)S(1)} %iota_compare_fusion.1, f32[1024,2048]{1,0:T(8,128)} %fusion.55, f32[2048]{0:T(1024)S(1)} %bitcast.122), kind=kOutput, calls=%fused_computation | convolution fusion | flops 8625586176 | bytes 20980740 | tf_op jit(solution)/shard_map/sf,sd->fd/dot_general | solution.py:118
  689.2 15.5 %multiply_convert_fusion.1 = bf16[2048,2048]{1,0:T(8,128)(2,1)} fusion(f32[]{:T(128)S(6)} %div.63, bf16[1024,2048]{1,0:T(8,128)(2,1)} %copy-done.38, f32[2048]{0:T(1024)S(1)} %bitcast.119, f32[2048]{0:T(1024)S(1)} %bitcast.113, f32[1024]{0:T(1024)S(1)} %fusion.48, bf16[1024,2048]{1,0:T(8,128)(2,1)} %all-reduce.6.cloned.1.call-done, ...), kind=kOutput, calls=%fused_computation.1 | convolution fusion | flops 8617197568 | bytes 21004292 | tf_op jit(solution)/shard_map/sd,sf->df/dot_general | solution.py:128
  706.6 12.6 %multiply_convert_fusion.3 = bf16[2048,3,512]{2,0,1:T(8,128)(2,1)} fusion(f32[]{:T(128)S(6)} %div.63, bf16[1024,1,512]{2,0,1:T(8,128)(2,1)S(1)} %copy-done.16, bf16[1024,1,512]{2,0,1:T(8,128)(2,1)S(1)} %copy-done.19, bf16[1024,1,512]{2,0,1:T(8,128)(2,1)S(1)} %copy-done.17, bf16[1024,2048]{1,0:T(8,128)(2,1)} %param.15, f32[2048]{0:T(1024)S(1)} %bitcast.117, ...), kind=kOutput, calls=%fused_computation.9 | convolution fusion | flops 6470762496 | bytes 13656068 | tf_op jit(solution)/shard_map/sd,sce->dce/dot_general | solution.py:169
  724.0 238.4 %all-reduce.10.cloned.1.call-done = (bf16[1024,2048]{1,0:T(8,128)(2,1)}, bf16[1024,2048]{1,0:T(8,128)(2,1)}) async-done(((bf16[1024,2048]{1,0:T(8,128)(2,1)}, bf16[1024,2048]{1,0:T(8,128)(2,1)}), (bf16[1024,2048]{1,0:T(8,128)(2,1)}, bf16[1024,2048]{1,0:T(8,128)(2,1)})) %all-reduce.10.cloned.1.call-update) | async-done | bytes 8388624 | tf_op jit(solution)/shard_map/psum | solution.py:108
  962.3 5.5 convert_reduce_fusion
  968.3 4.5 fusion.22
  972.8 25.3 %all-reduce = f32[8,1920]{1,0:T(8,128)S(1)} all-reduce(f32[8,1920]{1,0:T(8,128)S(1)} %constant_dynamic-update-slice_fusion), channel_id=7, replica_groups=mesh['dp'=8,'mp'=4] {'dp'}, use_global_device_ids=true, to_apply=%region_30.31.clone | all-reduce | flops 15360 | bytes 122880
  999.5 36.7 %reduce-scatter.11.cloned.1.call-done = bf16[2048,256]{1,0:T(8,128)(2,1)} async-done(((bf16[2048,2048]{1,0:T(8,128)(2,1)}), bf16[2048,256]{1,0:T(8,128)(2,1)}) %reduce-scatter.11.cloned.1.call-update) | async-done | bytes 1048592 | tf_op jit(solution)/shard_map/reduce_scatter | solution.py:200
  1036.3 2.7 convert_element_type.148
  1039.0 72.7 %reduce-scatter.9.cloned.1.call-done = bf16[256,2048]{1,0:T(8,128)(2,1)} async-done(((bf16[2048,2048]{1,0:T(8,128)(2,1)}), bf16[256,2048]{1,0:T(8,128)(2,1)}) %reduce-scatter.9.cloned.1.call-update) | async-done | bytes 1048592 | tf_op jit(solution)/shard_map/reduce_scatter | solution.py:200
  1111.7 2.8 convert_element_type.146
  1115.8 17.6 %add_add_fusion.2 = (f32[1024,2048]{1,0:T(8,128)}, bf16[1024,2048]{1,0:T(8,128)(2,1)}) fusion(f32[1024,2048]{1,0:T(8,128)} %copy-done.9, bf16[1024,2048]{1,0:T(8,128)(2,1)} %param.15, bf16[1024,2048]{1,0:T(8,128)(2,1)} %get-tuple-element.27, f32[1024]{0:T(1024)S(1)} %negate_multiply_fusion, f32[1024]{0:T(1024)S(1)} %multiply_multiply_fusion.2, ...), kind=kLoop, calls=%fused_computation.46 | loop fusion | flops 35651584 | bytes 37789696 | tf_op jit(solution)/shard_map/add | solution.py:176
  1133.4 43.3 %reduce-scatter.5.cloned.1.call-done = bf16[256,3,512]{2,0,1:T(8,128)(2,1)} async-done(((bf16[2048,3,512]{2,0,1:T(8,128)(2,1)}), bf16[256,3,512]{2,0,1:T(8,128)(2,1)}) %reduce-scatter.5.cloned.1.call-update) | async-done | bytes 786448 | tf_op jit(solution)/shard_map/reduce_scatter | solution.py:200
  1176.7 2.5 convert_element_type.142
  (178 shorter events, 33.3 us)
Async XLA Ops:
  7.2 52.8 %all-gather.7.cloned.1.call-start = ((), (), s32[]{:S(2)}) async-start(), calls=%async_computation.4 | async-start | bytes 7077888 | tf_op jit(solution)/shard_map/all_gather | solution.py:51
  9.5 92.7 %all-gather.9.cloned.1.call-start = ((), (), s32[]{:S(2)}) async-start(), calls=%async_computation.5 | async-start | bytes 2359296 | tf_op jit(solution)/shard_map/all_gather | solution.py:52
  10.3 253.4 %all-reduce.6.cloned.1.call-start = ((), (), s32[]{:S(2)}) async-start(), calls=%async_computation.6 | async-start | bytes 8388608 | tf_op jit(solution)/shard_map/psum | solution.py:101
  17.1 14.9 %copy-start = (bf16[1024,2048]{1,0:T(8,128)(2,1)S(1)}, bf16[1024,2048]{1,0:T(8,128)(2,1)}, u32[]{:S(2)}) copy-start(bf16[1024,2048]{1,0:T(8,128)(2,1)} %param.15) | copy-start | bytes 12582916
  32.0 38.4 %copy-start.22 = (f32[1024]{0:T(1024)}, f32[1024]{0:T(1024)S(1)}, u32[]{:S(2)}) copy-start(f32[1024]{0:T(1024)S(1)} %broadcast_multiply_fusion.8) | copy-start | bytes 12292
  33.3 37.1 %copy-start.24 = (f32[1024]{0:T(1024)}, f32[1024]{0:T(1024)S(1)}, u32[]{:S(2)}) copy-start(f32[1024]{0:T(1024)S(1)} %fusion.47) | copy-start | bytes 12292
  33.6 38.7 %copy-start.29 = (f32[4,128]{1,0:T(4,128)}, f32[4,128]{1,0:T(4,128)S(1)}, u32[]{:S(2)}) copy-start(f32[4,128]{1,0:T(4,128)S(1)} %add.148) | copy-start | bytes 6148
  33.9 36.6 %copy-start.31 = (f32[1,2,8,128]{3,1,2,0:T(2,128)}, f32[1,2,8,128]{3,1,2,0:T(2,128)S(1)}, u32[]{:S(2)}) copy-start(f32[1,2,8,128]{3,1,2,0:T(2,128)S(1)} %copy.87) | copy-start | bytes 24580
  33.9 36.6 %copy-start.20 = (f32[1,2,8,128]{3,1,2,0:T(2,128)}, f32[1,2,8,128]{3,1,2,0:T(2,128)S(1)}, u32[]{:S(2)}) copy-start(f32[1,2,8,128]{3,1,2,0:T(2,128)S(1)} %copy.86) | copy-start | bytes 24580
  70.6 9.3 copy-start.12
  72.3 7.7 copy-start.10
  97.6 3.2 copy-start.6
  102.2 7.3 copy-start.36
  108.3 210.4 %all-gather.11.cloned.1.call-start = ((), (), s32[]{:S(2)}) async-start(), calls=%async_computation.7 | async-start | bytes 9437184 | tf_op jit(solution)/shard_map/all_gather | solution.py:53
  108.9 267.4 %all-gather.13.cloned.1.call-start = ((), (), s32[]{:S(2)}) async-start(), calls=%async_computation.8 | async-start | bytes 9437184 | tf_op jit(solution)/shard_map/all_gather | solution.py:54
  109.4 467.5 %all-reduce.8.cloned.1.call-start = ((), (), s32[]{:S(2)}) async-start(), calls=%async_computation.9 | async-start | bytes 8388608 | tf_op jit(solution)/shard_map/psum | solution.py:132
  109.5 209.1 %copy-start.34 = (f32[1,2,8,128]{3,1,2,0:T(2,128)}, f32[1,2,8,128]{3,1,2,0:T(2,128)S(1)}, u32[]{:S(2)}) copy-start(f32[1,2,8,128]{3,1,2,0:T(2,128)S(1)} %copy.90) | copy-start | bytes 24580
  263.6 5.0 copy-start.1
  263.7 5.9 copy-start.4
  396.8 2.0 copy-start.38
  421.8 300.4 %reduce-scatter.7.cloned.1.call-start = ((), (), s32[]{:S(2)}) async-start(), calls=%async_computation.11 | async-start | bytes 2359296 | tf_op jit(solution)/shard_map/reduce_scatter | solution.py:200
  577.0 7.7 copy-start.2
  577.0 7.7 copy-start.5
  577.0 8.3 copy-start.8
  584.6 6.2 copy-start.15
  596.5 3.2 copy-start.9
  603.3 359.0 %all-reduce.10.cloned.1.call-start = ((), (), s32[]{:S(2)}) async-start(), calls=%async_computation.14 | async-start | bytes 16777216 | tf_op jit(solution)/shard_map/psum | solution.py:108
  610.2 28.2 %slice-start = ((s8[8388608]{0:T(1024)(128)(4,1)}), s8[4194304]{0:T(1024)(128)(4,1)S(1)}, s32[]{:S(2)}) async-start(s8[8388608]{0:T(1024)(128)(4,1)} %bitcast.80), calls=%async_computation.15 | async-start | bytes 8388608
  622.4 15.9 %slice-start.1 = ((s8[8388608]{0:T(1024)(128)(4,1)}), s8[4194304]{0:T(1024)(128)(4,1)S(1)}, s32[]{:S(2)}) async-start(s8[8388608]{0:T(1024)(128)(4,1)} %bitcast.80), calls=%async_computation.16 | async-start | bytes 8388608
  638.4 7.1 copy-start.13
  642.9 11.2 copy-start.11
  642.9 11.2 copy-start.30
  660.9 11.0 copy-start.18
  672.0 364.3 %reduce-scatter.11.cloned.1.call-start = ((), (), s32[]{:S(2)}) async-start(), calls=%async_computation.13 | async-start | bytes 9437184 | tf_op jit(solution)/shard_map/reduce_scatter | solution.py:200
  688.5 423.2 %reduce-scatter.9.cloned.1.call-start = ((), (), s32[]{:S(2)}) async-start(), calls=%async_computation.12 | async-start | bytes 9437184 | tf_op jit(solution)/shard_map/reduce_scatter | solution.py:200
  704.7 1.9 copy-start.19
  704.7 1.9 copy-start.21
  704.7 1.9 copy-start.23
  704.7 1.9 copy-start.25
  704.7 1.9 copy-start.32
  704.7 14.5 %copy-start.28 = (f32[1,2,8,128]{3,2,1,0:T(8,128)S(1)}, f32[1,2,8,128]{3,2,1,0:T(8,128)}, u32[]{:S(2)}) copy-start(f32[1,2,8,128]{3,2,1,0:T(8,128)} %get-tuple-element.42) | copy-start | bytes 24580
  704.7 14.5 %copy-start.37 = (u32[32]{0:T(128)S(1)}, u32[32]{0:T(128)}, u32[]{:S(2)}) copy-start(u32[32]{0:T(128)} %constant.45) | copy-start | bytes 388
  704.8 15.1 %copy-start.33 = (f32[2048]{0:T(1024)S(1)}, f32[2048]{0:T(1024)}, u32[]{:S(2)}) copy-start(f32[2048]{0:T(1024)} %get-tuple-element.57) | copy-start | bytes 24580
  704.8 471.9 %reduce-scatter.5.cloned.1.call-start = ((), (), s32[]{:S(2)}) async-start(), calls=%async_computation.10 | async-start | bytes 7077888 | tf_op jit(solution)/shard_map/reduce_scatter | solution.py:200
  719.2 2.6 copy-start.14
  719.2 248.6 %copy-start.27 = (f32[1024]{0:T(1024)S(1)}, f32[1024]{0:T(1024)}, u32[]{:S(2)}) copy-start(f32[1024]{0:T(1024)} %copy-done.26) | copy-start | bytes 12292
  962.3 5.5 copy-start.3
  962.3 5.9 copy-start.7
  (4 other events, 4.1 us)
Sparse Core Ops, SparseCore 0:
  10.4 49.4 all-gather.6
  61.8 28.0 all-gather.8
  108.4 155.2 all-reduce.5
  265.4 53.2 all-gather.10
  320.4 55.8 all-gather.12
  422.0 154.9 all-reduce.7
  603.5 40.0 reduce-scatter.6
  672.1 290.1 all-reduce.9
  965.8 70.4 reduce-scatter.10
  1040.2 71.4 reduce-scatter.8
  1115.1 61.6 reduce-scatter.4
where the time goes:
time: 1200 us; the launch traced here: 1190 us
  waiting for transfers between devices  797 us (66%)
  matrix products  197 us (16%)
  other arithmetic  103 us (9%)
  blocking collectives  36.5 us (3%)
  local copies, waits for them, and re-layouts  35.8 us (3%)
  between operations  16.4 us (1%)
    psum x1, waiting for transfers between devices, shards(): lax.psum(ffn_part.astype(jnp.bfloat16), 'mp').astype(jnp.float32)  238 us
    reduce_scatter x4, waiting for transfers between devices, scatter(): lax.psum_scatter(low, 'dp', scatter_dimension=axis, tiled=True)  153 us
    psum x1, waiting for transfers between devices, shards(): lax.psum(attn_part.astype(jnp.bfloat16), 'mp').astype(jnp.float32)  153 us
    psum x1, waiting for transfers between devices, shards(): lax.psum(two_part.astype(jnp.bfloat16), 'mp').astype(jnp.float32)  137 us
    all_gather x1, waiting for transfers between devices, shards(): whole_fc1 = lax.all_gather(w_fc1, 'dp', axis=0, tiled=True)  46.6 us
    all_gather x1, waiting for transfers between devices, shards(): whole_fc2 = lax.all_gather(w_fc2, 'dp', axis=1, tiled=True)  41.4 us
    all_gather x1, waiting for transfers between devices, shards(): whole_qkv = lax.all_gather(w_qkv, 'dp', axis=0, tiled=True)  26.1 us
    unnamed x1, blocking collectives  25.3 us
  transfers between devices with their start and end apart: 11, of which 9 were waited for; matrix products, arithmetic and copies ran while one was open for 21% of the time, Pallas kernels for 0%

commit v1 on v0

--- a/solution.py
+++ b/solution.py
@@ -98,7 +98,9 @@
     )
     attn_part = jnp.dot(mixed_heads, whole_out, preferred_element_type=jnp.float32)
     residual = (
-        inputs + lax.psum(attn_part.astype(jnp.bfloat16), "mp").astype(jnp.float32) + bias_out
+        inputs
+        + jnp.sum(lax.all_gather(attn_part.astype(jnp.bfloat16), "mp"), axis=0).astype(jnp.float32)
+        + bias_out
     )
     normed_two = layer_norm(residual, gain_two, shift_two).astype(jnp.bfloat16)
     preact = jnp.dot(normed_two, whole_fc1, preferred_element_type=jnp.float32) + bias_fc1

time: 1200 us -> 1320 us (1.10)
  waiting for transfers between devices: 797 us -> 915 us
    all_gather x0 -> x1, waiting for transfers between devices: none -> 285 us  [shards(): lax.all_gather(attn_part.astype(jnp.bfloat16), 'mp')]
    psum x1 -> x0, waiting for transfers between devices: 153 us -> none  [shards(): lax.psum(attn_part.astype(jnp.bfloat16), 'mp').astype(jnp.float32)]
    all_gather x1, waiting for transfers between devices: 46.6 us -> 33.4 us  [shards(): whole_fc1 = lax.all_gather(w_fc1, 'dp', axis=0, tiled=True)]
  transfers between devices with their start and end apart: 11 -> 11, of which waited for: 9 -> 9; matrix products, arithmetic and copies ran while one was open for 21% -> 20% of each run, Pallas kernels for 0% -> 0%
where the time goes in v1:
time: 1320 us; the launch traced here: 1310 us
  waiting for transfers between devices  915 us (69%)
  matrix products  187 us (14%)
  other arithmetic  115 us (9%)
  blocking collectives  36.5 us (3%)
  local copies, waits for them, and re-layouts  35.7 us (3%)
  between operations  16.4 us (1%)
    all_gather x1, waiting for transfers between devices, shards(): lax.all_gather(attn_part.astype(jnp.bfloat16), 'mp')  285 us
    psum x1, waiting for transfers between devices, shards(): lax.psum(ffn_part.astype(jnp.bfloat16), 'mp').astype(jnp.float32)  238 us
    reduce_scatter x4, waiting for transfers between devices, scatter(): lax.psum_scatter(low, 'dp', scatter_dimension=axis, tiled=True)  153 us
    psum x1, waiting for transfers between devices, shards(): lax.psum(two_part.astype(jnp.bfloat16), 'mp').astype(jnp.float32)  137 us
    all_gather x1, waiting for transfers between devices, shards(): whole_fc2 = lax.all_gather(w_fc2, 'dp', axis=1, tiled=True)  41.4 us
    all_gather x1, waiting for transfers between devices, shards(): whole_fc1 = lax.all_gather(w_fc1, 'dp', axis=0, tiled=True)  33.4 us
  transfers between devices with their start and end apart: 11, of which 9 were waited for; matrix products, arithmetic and copies ran while one was open for 20% of the time, Pallas kernels for 0%

profile of v1, /device:TPU:0, one launch (start us, length us, event | category | flops | bytes accessed | tf_op | source)
XLA Modules:
  0.0 1306.8 jit_solution(17185313752995946794)
XLA Ops:
  7.2 2.3 copy.59
  17.1 11.2 all-gather.2
  29.2 2.8 convert_reduce_fusion.2
  33.9 26.1 %all-gather.9.cloned.1.call-done = bf16[2048,3,512]{0,2,1:T(8,128)(2,1)} async-done(((bf16[256,3,512]{0,2,1:T(8,128)(2,1)}), bf16[2048,3,512]{0,2,1:T(8,128)(2,1)}) %all-gather.9.cloned.1.call-update) | async-done | bytes 6291472 | tf_op jit(solution)/shard_map/all_gather | solution.py:51
  60.0 10.4 fusion.43
  72.3 7.7 fusion.62
  80.0 8.1 fusion
  90.1 7.4 divide_convert_fusion
  97.5 3.2 copy-done.6
  102.2 6.0 convolution_convert_fusion.2
  110.8 284.6 %all-gather.17.cloned.1.call-done = bf16[4096,2048]{1,0:T(8,128)(2,1)} async-done(((bf16[1024,2048]{1,0:T(8,128)(2,1)}), bf16[4096,2048]{1,0:T(8,128)(2,1)}) %all-gather.17.cloned.1.call-update) | async-done | bytes 16777232 | tf_op jit(solution)/shard_map/all_gather | solution.py:102
  395.3 12.4 reduce_sum.203
  407.8 5.0 fusion.26
  413.7 2.4 multiply_reduce_fusion.1
  416.1 33.4 %all-gather.13.cloned.1.call-done = bf16[2048,2048]{1,0:T(8,128)(2,1)} async-done(((bf16[256,2048]{1,0:T(8,128)(2,1)}), bf16[2048,2048]{1,0:T(8,128)(2,1)}) %all-gather.13.cloned.1.call-update) | async-done | bytes 8388624 | tf_op jit(solution)/shard_map/all_gather | solution.py:53
  449.6 16.2 %fusion.55 = f32[1024,2048]{1,0:T(8,128)} fusion(bf16[2048,2048]{1,0:T(8,128)(2,1)} %all-gather.13.cloned.1.call-done, f32[2048]{0:T(1024)S(1)} %bitcast.120, f32[2048]{0:T(1024)S(1)} %bitcast.111, f32[1024]{0:T(1024)S(1)} %fusion.48, bf16[1024,2048]{1,0:T(8,128)(2,1)} %reduce_sum.203, bf16[1024,2048]{1,0:T(8,128)(2,1)} %param.15, ...), kind=kOutput, calls=%fused_computation.131 | convolution fusion | flops 8608808960 | bytes 25198592 | tf_op jit(solution)/shard_map/dot_general | solution.py:106
  465.7 41.4 %all-gather.15.cloned.1.call-done = bf16[2048,2048]{1,0:T(8,128)(2,1)} async-done(((bf16[2048,256]{1,0:T(8,128)(2,1)}), bf16[2048,2048]{1,0:T(8,128)(2,1)}) %all-gather.15.cloned.1.call-update) | async-done | bytes 8388624 | tf_op jit(solution)/shard_map/all_gather | solution.py:54
  507.2 20.7 %fusion.63 = (f32[2048]{0:T(1024)}, bf16[1024,2048]{1,0:T(8,128)(2,1)S(1)}) fusion(f32[1024,2048]{1,0:T(8,128)} %fusion.55, f32[2048]{0:T(1024)S(1)} %bitcast.122, bf16[2048,2048]{1,0:T(8,128)(2,1)} %all-gather.15.cloned.1.call-done, bf16[1024,2048]{1,0:T(8,128)(2,1)} %param.16, pred[1024]{0:T(1024)(128)(4,1)S(1)} %iota_compare_fusion.1), kind=kOutput, calls=%fused_computation.137 | convolution fusion | flops 8642361344 | bytes 25183232 | tf_op jit(solution)/shard_map/sd,fd->sf/dot_general | solution.py:124
  529.9 12.6 convolution_convert_fusion
  544.0 17.2 %convolution_convert_fusion.1 = bf16[1024,2048]{1,0:T(8,128)(2,1)} fusion(bf16[2048,2048]{1,0:T(8,128)(2,1)} %all-gather.15.cloned.1.call-done, f32[1024,2048]{1,0:T(8,128)} %fusion.55, f32[2048]{0:T(1024)S(1)} %bitcast.123), kind=kOutput, calls=%fused_computation.62 | convolution fusion | flops 8613003264 | bytes 20979712 | tf_op jit(solution)/shard_map/dot_general | solution.py:108
  561.2 136.6 %all-reduce.5.cloned.1.call-done = bf16[1024,2048]{1,0:T(8,128)(2,1)} async-done(((bf16[1024,2048]{1,0:T(8,128)(2,1)}), bf16[1024,2048]{1,0:T(8,128)(2,1)}) %all-reduce.5.cloned.1.call-update) | async-done | bytes 4194320 | tf_op jit(solution)/shard_map/psum | solution.py:134
  697.7 7.6 convert_reduce_fusion.1
  706.0 5.5 fusion.21
  711.5 5.7 fusion.59
  717.2 3.2 copy-done.9
  720.4 3.6 multiply_convert_fusion.5
  724.3 6.3 fusion.39
  730.6 12.3 multiply_reduce_fusion
  742.9 16.0 %multiply_convert_fusion.2 = bf16[4,1024,1024]{1,2,0:T(8,128)(2,1)} fusion(f32[4,1024,1024]{1,2,0:T(8,128)} %get-tuple-element.54, f32[4,1024,1024]{1,2,0:T(8,128)} %get-tuple-element.50, f32[4,1024]{1,0:T(4,128)S(1)} %get-tuple-element.53, f32[4,1024]{1,0:T(4,128)S(1)} %log_add_fusion), kind=kLoop, calls=%fused_computation.2 | loop fusion | flops 16777216 | bytes 41975808 | tf_op jit(solution)/shard_map/convert_element_type | solution.py:156
  758.9 4.6 bitcast_convert_fusion.1
  763.5 2.4 copy.71
  765.9 6.4 bitcast_convert_fusion.2
  774.6 6.3 multiply_convert_fusion.6
  781.4 11.1 bitcast_convert_fusion
  792.6 16.5 %multiply_convert_fusion = bf16[2048,2048]{1,0:T(8,128)(2,1)} fusion(f32[]{:T(128)S(6)} %div.63, bf16[1024,2048]{1,0:T(8,128)(2,1)} %param.16, pred[1024]{0:T(1024)(128)(4,1)S(1)} %iota_compare_fusion.1, f32[1024,2048]{1,0:T(8,128)} %fusion.55, f32[2048]{0:T(1024)S(1)} %bitcast.124), kind=kOutput, calls=%fused_computation | convolution fusion | flops 8625586176 | bytes 20980740 | tf_op jit(solution)/shard_map/sf,sd->fd/dot_general | solution.py:120
  809.8 15.5 %multiply_convert_fusion.1 = bf16[2048,2048]{1,0:T(8,128)(2,1)} fusion(f32[]{:T(128)S(6)} %div.63, bf16[1024,2048]{1,0:T(8,128)(2,1)} %copy-done.38, f32[2048]{0:T(1024)S(1)} %bitcast.121, f32[2048]{0:T(1024)S(1)} %bitcast.115, f32[1024]{0:T(1024)S(1)} %fusion.48, bf16[1024,2048]{1,0:T(8,128)(2,1)} %reduce_sum.203, bf16[1024,2048]{1,0:T(8,128)(2,1)} %param.15, ...), kind=kOutput, calls=%fused_computation.1 | convolution fusion | flops 8617197568 | bytes 21004292 | tf_op jit(solution)/shard_map/sd,sf->df/dot_general | solution.py:130
  827.2 12.6 multiply_convert_fusion.3
  844.6 238.3 %all-reduce.7.cloned.1.call-done = (bf16[1024,2048]{1,0:T(8,128)(2,1)}, bf16[1024,2048]{1,0:T(8,128)(2,1)}) async-done(((bf16[1024,2048]{1,0:T(8,128)(2,1)}, bf16[1024,2048]{1,0:T(8,128)(2,1)}), (bf16[1024,2048]{1,0:T(8,128)(2,1)}, bf16[1024,2048]{1,0:T(8,128)(2,1)})) %all-reduce.7.cloned.1.call-update) | async-done | bytes 8388624 | tf_op jit(solution)/shard_map/psum | solution.py:110
  1082.9 5.5 convert_reduce_fusion
  1088.8 4.5 fusion.22
  1093.4 25.3 %all-reduce = f32[8,1920]{1,0:T(8,128)S(1)} all-reduce(f32[8,1920]{1,0:T(8,128)S(1)} %constant_dynamic-update-slice_fusion), channel_id=8, replica_groups=mesh['dp'=8,'mp'=4] {'dp'}, use_global_device_ids=true, to_apply=%region_30.31.clone | all-reduce | flops 15360 | bytes 122880
  1120.1 36.7 %reduce-scatter.11.cloned.1.call-done = bf16[2048,256]{1,0:T(8,128)(2,1)} async-done(((bf16[2048,2048]{1,0:T(8,128)(2,1)}), bf16[2048,256]{1,0:T(8,128)(2,1)}) %reduce-scatter.11.cloned.1.call-update) | async-done | bytes 1048592 | tf_op jit(solution)/shard_map/reduce_scatter | solution.py:202
  1156.8 2.7 convert_element_type.150
  1159.6 72.7 %reduce-scatter.9.cloned.1.call-done = bf16[256,2048]{1,0:T(8,128)(2,1)} async-done(((bf16[2048,2048]{1,0:T(8,128)(2,1)}), bf16[256,2048]{1,0:T(8,128)(2,1)}) %reduce-scatter.9.cloned.1.call-update) | async-done | bytes 1048592 | tf_op jit(solution)/shard_map/reduce_scatter | solution.py:202
  1232.3 2.8 convert_element_type.148
  1236.4 17.6 %add_add_fusion.2 = (f32[1024,2048]{1,0:T(8,128)}, bf16[1024,2048]{1,0:T(8,128)(2,1)}) fusion(f32[1024,2048]{1,0:T(8,128)} %copy-done.9, bf16[1024,2048]{1,0:T(8,128)(2,1)} %param.15, bf16[1024,2048]{1,0:T(8,128)(2,1)} %get-tuple-element.27, f32[1024]{0:T(1024)S(1)} %negate_multiply_fusion, f32[1024]{0:T(1024)S(1)} %multiply_multiply_fusion.2, ...), kind=kLoop, calls=%fused_computation.46 | loop fusion | flops 35651584 | bytes 37789696 | tf_op jit(solution)/shard_map/add | solution.py:178
  1253.9 43.4 %reduce-scatter.5.cloned.1.call-done = bf16[256,3,512]{2,0,1:T(8,128)(2,1)} async-done(((bf16[2048,3,512]{2,0,1:T(8,128)(2,1)}), bf16[256,3,512]{2,0,1:T(8,128)(2,1)}) %reduce-scatter.5.cloned.1.call-update) | async-done | bytes 786448 | tf_op jit(solution)/shard_map/reduce_scatter | solution.py:202
  1297.3 2.5 convert_element_type.144
  (179 shorter events, 35.3 us)
Async XLA Ops:
  7.2 52.8 %all-gather.9.cloned.1.call-start = ((), (), s32[]{:S(2)}) async-start(), calls=%async_computation.4 | async-start | bytes 7077888 | tf_op jit(solution)/shard_map/all_gather | solution.py:51
  9.5 92.6 %all-gather.11.cloned.1.call-start = ((), (), s32[]{:S(2)}) async-start(), calls=%async_computation.5 | async-start | bytes 2359296 | tf_op jit(solution)/shard_map/all_gather | solution.py:52
  10.3 385.0 %all-gather.17.cloned.1.call-start = ((), (), s32[]{:S(2)}) async-start(), calls=%async_computation.13 | async-start | bytes 20971520 | tf_op jit(solution)/shard_map/all_gather | solution.py:102
  17.1 14.9 %copy-start = (bf16[1024,2048]{1,0:T(8,128)(2,1)S(1)}, bf16[1024,2048]{1,0:T(8,128)(2,1)}, u32[]{:S(2)}) copy-start(bf16[1024,2048]{1,0:T(8,128)(2,1)} %param.15) | copy-start | bytes 12582916
  32.0 38.4 %copy-start.22 = (f32[1024]{0:T(1024)}, f32[1024]{0:T(1024)S(1)}, u32[]{:S(2)}) copy-start(f32[1024]{0:T(1024)S(1)} %broadcast_multiply_fusion.8) | copy-start | bytes 12292
  33.3 37.1 %copy-start.24 = (f32[1024]{0:T(1024)}, f32[1024]{0:T(1024)S(1)}, u32[]{:S(2)}) copy-start(f32[1024]{0:T(1024)S(1)} %fusion.47) | copy-start | bytes 12292
  33.6 38.7 %copy-start.29 = (f32[4,128]{1,0:T(4,128)}, f32[4,128]{1,0:T(4,128)S(1)}, u32[]{:S(2)}) copy-start(f32[4,128]{1,0:T(4,128)S(1)} %add.146) | copy-start | bytes 6148
  33.9 36.6 %copy-start.31 = (f32[1,2,8,128]{3,1,2,0:T(2,128)}, f32[1,2,8,128]{3,1,2,0:T(2,128)S(1)}, u32[]{:S(2)}) copy-start(f32[1,2,8,128]{3,1,2,0:T(2,128)S(1)} %copy.87) | copy-start | bytes 24580
  33.9 36.6 %copy-start.20 = (f32[1,2,8,128]{3,1,2,0:T(2,128)}, f32[1,2,8,128]{3,1,2,0:T(2,128)S(1)}, u32[]{:S(2)}) copy-start(f32[1,2,8,128]{3,1,2,0:T(2,128)S(1)} %copy.86) | copy-start | bytes 24580
  70.6 9.3 copy-start.12
  72.3 7.7 copy-start.10
  97.5 3.2 copy-start.6
  102.2 7.3 copy-start.36
  108.2 341.4 %all-gather.13.cloned.1.call-start = ((), (), s32[]{:S(2)}) async-start(), calls=%async_computation.6 | async-start | bytes 9437184 | tf_op jit(solution)/shard_map/all_gather | solution.py:53
  108.8 398.4 %all-gather.15.cloned.1.call-start = ((), (), s32[]{:S(2)}) async-start(), calls=%async_computation.7 | async-start | bytes 9437184 | tf_op jit(solution)/shard_map/all_gather | solution.py:54
  109.4 588.4 %all-reduce.5.cloned.1.call-start = ((), (), s32[]{:S(2)}) async-start(), calls=%async_computation.8 | async-start | bytes 8388608 | tf_op jit(solution)/shard_map/psum | solution.py:134
  109.4 340.1 %copy-start.34 = (f32[1,2,8,128]{3,1,2,0:T(2,128)}, f32[1,2,8,128]{3,1,2,0:T(2,128)S(1)}, u32[]{:S(2)}) copy-start(f32[1,2,8,128]{3,1,2,0:T(2,128)S(1)} %copy.90) | copy-start | bytes 24580
  407.8 5.0 copy-start.1
  407.8 5.9 copy-start.4
  527.9 2.1 copy-start.38
  542.6 300.3 %reduce-scatter.7.cloned.1.call-start = ((), (), s32[]{:S(2)}) async-start(), calls=%async_computation.10 | async-start | bytes 2359296 | tf_op jit(solution)/shard_map/reduce_scatter | solution.py:202
  697.7 7.7 copy-start.2
  697.7 7.7 copy-start.5
  697.7 8.3 copy-start.8
  705.4 6.1 copy-start.15
  717.2 3.2 copy-start.9
  724.1 358.9 %all-reduce.7.cloned.1.call-start = ((), (), s32[]{:S(2)}) async-start(), calls=%async_computation.14 | async-start | bytes 16777216 | tf_op jit(solution)/shard_map/psum | solution.py:110
  730.6 28.2 %slice-start = ((s8[8388608]{0:T(1024)(128)(4,1)}), s8[4194304]{0:T(1024)(128)(4,1)S(1)}, s32[]{:S(2)}) async-start(s8[8388608]{0:T(1024)(128)(4,1)} %bitcast.81), calls=%async_computation.15 | async-start | bytes 8388608
  742.9 16.0 %slice-start.1 = ((s8[8388608]{0:T(1024)(128)(4,1)}), s8[4194304]{0:T(1024)(128)(4,1)S(1)}, s32[]{:S(2)}) async-start(s8[8388608]{0:T(1024)(128)(4,1)} %bitcast.81), calls=%async_computation.16 | async-start | bytes 8388608
  758.9 7.0 copy-start.13
  763.5 11.1 copy-start.11
  763.5 11.1 copy-start.30
  781.4 11.1 copy-start.18
  792.6 364.3 %reduce-scatter.11.cloned.1.call-start = ((), (), s32[]{:S(2)}) async-start(), calls=%async_computation.12 | async-start | bytes 9437184 | tf_op jit(solution)/shard_map/reduce_scatter | solution.py:202
  809.1 423.1 %reduce-scatter.9.cloned.1.call-start = ((), (), s32[]{:S(2)}) async-start(), calls=%async_computation.11 | async-start | bytes 9437184 | tf_op jit(solution)/shard_map/reduce_scatter | solution.py:202
  825.3 1.9 copy-start.19
  825.3 1.9 copy-start.21
  825.3 1.9 copy-start.23
  825.3 1.9 copy-start.25
  825.3 1.9 copy-start.32
  825.4 14.5 %copy-start.28 = (f32[1,2,8,128]{3,2,1,0:T(8,128)S(1)}, f32[1,2,8,128]{3,2,1,0:T(8,128)}, u32[]{:S(2)}) copy-start(f32[1,2,8,128]{3,2,1,0:T(8,128)} %get-tuple-element.42) | copy-start | bytes 24580
  825.4 14.5 %copy-start.37 = (u32[32]{0:T(128)S(1)}, u32[32]{0:T(128)}, u32[]{:S(2)}) copy-start(u32[32]{0:T(128)} %constant.47) | copy-start | bytes 388
  825.4 15.1 %copy-start.33 = (f32[2048]{0:T(1024)S(1)}, f32[2048]{0:T(1024)}, u32[]{:S(2)}) copy-start(f32[2048]{0:T(1024)} %get-tuple-element.57) | copy-start | bytes 24580
  825.4 471.9 %reduce-scatter.5.cloned.1.call-start = ((), (), s32[]{:S(2)}) async-start(), calls=%async_computation.9 | async-start | bytes 7077888 | tf_op jit(solution)/shard_map/reduce_scatter | solution.py:202
  839.8 2.6 copy-start.14
  839.8 248.6 %copy-start.27 = (f32[1024]{0:T(1024)S(1)}, f32[1024]{0:T(1024)}, u32[]{:S(2)}) copy-start(f32[1024]{0:T(1024)} %copy-done.26) | copy-start | bytes 12292
  1082.9 5.6 copy-start.3
  1082.9 5.9 copy-start.7
  (4 other events, 4.1 us)
Sparse Core Ops, SparseCore 0:
  10.4 49.4 all-gather.8
  61.8 28.0 all-gather.10
  108.3 286.9 all-gather.16
  397.1 52.4 all-gather.12
  451.3 55.8 all-gather.14
  542.7 154.9 all-reduce.4
  724.2 40.0 reduce-scatter.6
  792.7 290.1 all-reduce.6
  1086.4 70.4 reduce-scatter.10
  1160.7 71.4 reduce-scatter.8
  1235.6 61.6 reduce-scatter.4
